TPU v7x, 32 devices: a whole 2x2x4 slice. The times are simulated.
32 devices in a mesh: fsdp: 8 (over y, x, core), dp: 4 (over z).
Axes of the slice: x: 2, y: 2, z: 4, core: 2. Of those that a mesh axis runs over, the one named last changes fastest.
Arguments:
- tokens: bfloat16 [16384, 4096], P(('fsdp', 'dp')), may hold values from -40 to 40
- cotangent: bfloat16 [16384, 2048], P(('fsdp', 'dp')), may hold values from -20 to 20
- weight: bfloat16 [4096, 2048], P('fsdp'), may hold values from -1 to 1
- left_vector: float32 [4096], P('fsdp'), may hold values from -6 to 6
Outputs:
- layer_out: bfloat16 [16384, 2048], P(('fsdp', 'dp'))
- input_grad: bfloat16 [16384, 4096], P(('fsdp', 'dp'))
- update: bfloat16 [4096, 2048], P('fsdp')
- left_next: float32 [4096], P('fsdp')
- right_next: float32 [2048], replicated
All inputs are finite; a program needn't handle non-finite values.
Results may differ from a plain program's by a relative error of at most 0.015.
Values may be sent and summed in bfloat16 or wider, within the bound.
A program may use at most 128 MiB of HBM per device.

v0:
```python
import jax
import jax.numpy as jnp
from jax import lax
from jax.sharding import PartitionSpec as P

epsilon = 1e-06


def per_device(tokens, cotangent, weight, left_vector):
    highest = lax.Precision.HIGHEST
    weight_wide = weight.astype(jnp.float32)
    part_right = jnp.dot(left_vector, weight_wide, precision=highest)
    right_raw = lax.psum(part_right, "fsdp")
    right_next = right_raw / jnp.sqrt(jnp.sum(right_raw * right_raw) + epsilon)
    left_raw = jnp.dot(weight_wide, right_next, precision=highest)
    left_sq = lax.psum(jnp.sum(left_raw * left_raw), "fsdp")
    spectral = jnp.sqrt(left_sq + epsilon)
    left_next = left_raw / spectral
    gathered = lax.all_gather(weight, "fsdp", axis=0, tiled=True)
    product = jnp.dot(tokens, gathered, preferred_element_type=jnp.float32)
    layer_out = (product / spectral).astype(jnp.bfloat16)
    back_prod = lax.dot_general(
        cotangent, gathered, (((1,), (1,)), ((), ())), preferred_element_type=jnp.float32
    )
    input_grad = (back_prod / spectral).astype(jnp.bfloat16)
    shard_rows = weight.shape[0]
    shard_sum = lax.psum_scatter(
        lax.dot_general(
            tokens, cotangent, (((0,), (0,)), ((), ())), preferred_element_type=jnp.float32
        ).astype(jnp.bfloat16),
        "fsdp",
        scatter_dimension=0,
        tiled=True,
    )
    grad_sum = lax.psum(shard_sum, "dp").astype(jnp.float32)
    entry_count = shard_rows * lax.axis_size("fsdp") * weight.shape[1]
    along_right = jnp.dot(grad_sum, right_next, precision=highest)
    grad_sq_raw, inner_prod, cross_term = lax.psum(
        (
            jnp.sum(grad_sum * grad_sum),
            jnp.sum(grad_sum * weight_wide),
            jnp.sum(left_next * along_right),
        ),
        "fsdp",
    )
    rank_coeff = inner_prod / (spectral * spectral)
    gradient = grad_sum / spectral - rank_coeff * left_next[:, None] * right_next[None, :]
    left_unit = left_sq / (left_sq + epsilon)
    right_unit = jnp.sum(right_next * right_next)
    grad_sq = (
        grad_sq_raw / (spectral * spectral)
        - 2.0 * rank_coeff * cross_term / spectral
        + rank_coeff * rank_coeff * left_unit * right_unit
    )
    grad_rms = jnp.sqrt(grad_sq / entry_count + epsilon)
    update = (gradient / grad_rms).astype(jnp.bfloat16)
    return (layer_out, input_grad, update, left_next, right_next)


def solution(mesh):
    placed = (P(("fsdp", "dp"), None), P(("fsdp", "dp"), None), P("fsdp", None), P("fsdp"))
    return jax.shard_map(
        per_device,
        mesh=mesh,
        in_specs=placed,
        out_specs=(
            P(("fsdp", "dp"), None),
            P(("fsdp", "dp"), None),
            P("fsdp", None),
            P("fsdp"),
            P(),
        ),
        check_vma=False,
    )
```

profile of v0, /device:TPU:0, one launch (start us, length us, event | category | flops | bytes accessed | tf_op | source)
XLA Modules:
  0.0 355.8 jit_solution(14946485540148376440)
XLA Ops:
  7.2 0.0 copy-start
  7.2 0.0 reduce-scatter.2.cloned.1.call-start
  7.2 1.5 copy-done
  8.8 14.6 %convolution_convert_fusion = bf16[4096,2048]{1,0:T(8,128)(2,1)} fusion(bf16[512,4096]{1,0:T(8,128)(2,1)} %param.4, bf16[512,2048]{1,0:T(8,128)(2,1)S(1)} %copy-done), kind=kOutput, calls=%fused_computation | convolution fusion | flops 8598323200 | bytes 23068672 | tf_op jit(solution)/shard_map/dot_general | solution.py:28
  23.4 0.0 reduce-scatter.2.cloned.1.call-update
  23.4 0.0 copy-start.3
  23.4 0.0 all-reduce.3.cloned.1.call-start
  23.5 119.0 %reduce-scatter.2.cloned.1.call-done = bf16[512,2048]{1,0:T(8,128)(2,1)} async-done(((bf16[4096,2048]{1,0:T(8,128)(2,1)}), bf16[512,2048]{1,0:T(8,128)(2,1)}) %reduce-scatter.2.cloned.1.call-update) | async-done | bytes 2097168 | tf_op jit(solution)/shard_map/reduce_scatter | solution.py:27
  142.5 0.0 all-reduce.3.cloned.1.call-update
  142.5 0.0 all-gather.2.cloned.1.call-start
  142.5 0.7 all-gather.2.cloned.1.call-update
  143.2 0.0 copy-done.3
  143.2 2.5 fusion.5
  145.7 13.2 %psum.42 = f32[2048]{0:T(1024)S(1)} all-reduce(f32[2048]{0:T(1024)S(1)} %bitcast.20), channel_id=1, replica_groups=mesh['fsdp'=8,'dp'=4] {'fsdp'}, use_global_device_ids=true, to_apply=%region_0.0 | all-reduce | flops 2048 | bytes 16384 | tf_op jit(solution)/shard_map/psum | solution.py:13
  158.9 0.6 multiply_reduce_fusion.1
  160.2 0.6 multiply_reduce_fusion
  160.8 0.0 copy-start.1
  160.8 3.3 fusion.6
  164.1 0.6 multiply_reduce_fusion.3
  164.7 13.2 %psum.43 = f32[]{:T(128)} all-reduce(f32[]{:T(128)} %multiply_reduce_fusion.3), channel_id=1, replica_groups=mesh['fsdp'=8,'dp'=4] {'fsdp'}, use_global_device_ids=true, to_apply=%region_3.0 | all-reduce | flops 1 | bytes 8 | tf_op jit(solution)/shard_map/psum | solution.py:16
  179.3 51.7 %all-reduce.3.cloned.1.call-done = bf16[512,2048]{1,0:T(8,128)(2,1)} async-done(((bf16[512,2048]{1,0:T(8,128)(2,1)}), bf16[512,2048]{1,0:T(8,128)(2,1)}) %all-reduce.3.cloned.1.call-update) | async-done | bytes 2097168 | tf_op jit(solution)/shard_map/psum | solution.py:35
  231.0 3.3 fusion.7
  234.3 0.6 multiply_reduce_fusion.2
  235.0 4.0 %fusion.2 = (f32[]{:T(128)}, f32[]{:T(128)}) fusion(bf16[512,2048]{1,0:T(8,128)(2,1)} %all-reduce.3.cloned.1.call-done, bf16[512,2048]{1,0:T(8,128)(2,1)} %param.6), kind=kLoop, calls=%fused_computation.7 | loop fusion | flops 6291454 | bytes 4194312 | tf_op jit(solution)/shard_map/reduce_sum | solution.py:41
  239.0 15.1 %all-reduce = (f32[]{:T(128)}, f32[]{:T(128)}, f32[]{:T(128)}) all-reduce(f32[]{:T(128)} %get-tuple-element.6, f32[]{:T(128)} %get-tuple-element.5, f32[]{:T(128)} %get-tuple-element.12), channel_id=1, replica_groups=mesh['fsdp'=8,'dp'=4] {'fsdp'}, use_global_device_ids=true, to_apply=%region_9.0 | all-reduce | flops 3 | bytes 24 | tf_op jit(solution)/shard_map/psum | solution.py:38
  256.8 0.0 copy-done.1
  256.8 3.7 %fusion.4 = bf16[512,2048]{1,0:T(8,128)(2,1)} fusion(bf16[512,2048]{1,0:T(8,128)(2,1)} %all-reduce.3.cloned.1.call-done, f32[]{:T(128)S(6)} %sqrt.11, f32[2048]{0:T(1024)S(1)} %get-tuple-element.11, f32[512]{0:T(512)S(1)} %broadcast_multiply_fusion, f32[]{:T(128)S(6)} %sqrt.10), kind=kLoop, calls=%fused_computation.9 | loop fusion | flops 6291456 | bytes 4204552 | tf_op jit(solution)/shard_map/convert_element_type | solution.py:56
  260.5 0.0 copy-done.2
  260.5 61.3 %all-gather.2.cloned.1.call-done = bf16[4096,2048]{1,0:T(8,128)(2,1)} async-done(((bf16[512,2048]{1,0:T(8,128)(2,1)}), bf16[4096,2048]{1,0:T(8,128)(2,1)}) %all-gather.2.cloned.1.call-update) | async-done | bytes 16777232 | tf_op jit(solution)/shard_map/all_gather | solution.py:19
  321.8 13.9 %divide_convert_fusion = bf16[512,4096]{1,0:T(8,128)(2,1)} fusion(bf16[512,2048]{1,0:T(8,128)(2,1)S(1)} %copy-done, bf16[4096,2048]{1,0:T(8,128)(2,1)} %all-gather.2.cloned.1.call-done, f32[]{:T(128)S(6)} %sqrt.10), kind=kOutput, calls=%fused_computation.1 | convolution fusion | flops 8594128896 | bytes 23068676 | tf_op jit(solution)/shard_map/dot_general | solution.py:22
  335.7 0.0 copy-done.4
  335.7 13.5 %divide_convert_fusion.1 = bf16[512,2048]{1,0:T(8,128)(2,1)} fusion(bf16[512,4096]{1,0:T(8,128)(2,1)S(1)} %copy-done.4, bf16[4096,2048]{1,0:T(8,128)(2,1)} %all-gather.2.cloned.1.call-done, f32[]{:T(128)S(6)} %sqrt.10), kind=kOutput, calls=%fused_computation.10 | convolution fusion | flops 8592031744 | bytes 23068676 | tf_op jit(solution)/shard_map/dot_general | solution.py:20
  (3 shorter events, 0.0 us)
Async XLA Ops:
  7.2 1.6 copy-start
  7.2 135.3 %reduce-scatter.2.cloned.1.call-start = ((), (), s32[]{:S(2)}) async-start(), calls=%async_computation.2 | async-start | bytes 18874368 | tf_op jit(solution)/shard_map/reduce_scatter | solution.py:27
  23.4 119.8 %copy-start.3 = (f32[512]{0:T(512)S(1)}, f32[512]{0:T(512)}, u32[]{:S(2)}) copy-start(f32[512]{0:T(512)} %param.7) | copy-start | bytes 6148
  23.4 207.6 %all-reduce.3.cloned.1.call-start = ((), (), s32[]{:S(2)}) async-start(), calls=%async_computation.3 | async-start | bytes 4194304 | tf_op jit(solution)/shard_map/psum | solution.py:35
  142.5 179.3 %all-gather.2.cloned.1.call-start = ((), (), s32[]{:S(2)}) async-start(), calls=%async_computation.1 | async-start | bytes 18874368 | tf_op jit(solution)/shard_map/all_gather | solution.py:19
  160.8 96.0 %copy-start.1 = (f32[2048]{0:T(1024)}, f32[2048]{0:T(1024)S(1)}, u32[]{:S(2)}) copy-start(f32[2048]{0:T(1024)S(1)} %get-tuple-element.11) | copy-start | bytes 24580
  235.0 25.5 %copy-start.2 = (f32[512]{0:T(512)}, f32[512]{0:T(512)S(1)}, u32[]{:S(2)}) copy-start(f32[512]{0:T(512)S(1)} %get-tuple-element.13) | copy-start | bytes 6148
  321.8 13.9 %copy-start.4 = (bf16[512,4096]{1,0:T(8,128)(2,1)S(1)}, bf16[512,4096]{1,0:T(8,128)(2,1)}, u32[]{:S(2)}) copy-start(bf16[512,4096]{1,0:T(8,128)(2,1)} %param.4) | copy-start | bytes 12582916
Sparse Core Ops, SparseCore 0:
  23.5 118.8 reduce-scatter.1
  144.8 86.1 all-reduce.2
  232.9 88.8 all-gather.1
where the time goes:
time: 356 us
  waiting for transfers between devices  233 us (65%)
  matrix products  51.2 us (14%)
  blocking collectives  41.4 us (12%)
  between operations  18.5 us (5%)
  other arithmetic  10.2 us (3%)
    reduce_scatter x1, waiting for transfers between devices, per_device(): lax.psum_scatter(lax.dot_general(tokens, cotangent, (((0,), (0,)), ((), (...  119 us
    all_gather x1, waiting for transfers between devices, per_device(): gathered = lax.all_gather(weight, 'fsdp', axis=0, tiled=True)  61.3 us
    psum x1, waiting for transfers between devices, per_device(): grad_sum = lax.psum(shard_sum, 'dp').astype(jnp.float32)  51.7 us
    psum x1, blocking collectives, per_device(): lax.psum((jnp.sum(grad_sum * grad_sum), jnp.sum(grad_sum * weight_wide),...  15.1 us
    dot_general x1, matrix products, per_device(): lax.dot_general(tokens, cotangent, (((0,), (0,)), ((), ())), preferred_el...  14.6 us
    dot_general x1, matrix products, per_device(): lax.dot_general(cotangent, gathered, (((1,), (1,)), ((), ())), preferred_...  13.9 us
    dot_general x1, matrix products, per_device(): product = jnp.dot(tokens, gathered, preferred_element_type=jnp.float32)  13.5 us
    psum x1, blocking collectives, per_device(): left_sq = lax.psum(jnp.sum(left_raw * left_raw), 'fsdp')  13.2 us
  transfers between devices with their start and end apart: 3, of which 3 were waited for; matrix products, arithmetic and copies ran while one was open for 5% of the time, Pallas kernels for 0%

commit v1 on v0

--- a/solution.py
+++ b/solution.py
@@ -4,6 +4,12 @@
 from jax.sharding import PartitionSpec as P
 
 epsilon = 1e-06
+
+
+def add_all(array, axis):
+    blocks = lax.all_gather(array, axis, axis=0, tiled=False)
+    total = blocks.sum(axis=0)
+    return total
 
 
 def per_device(tokens, cotangent, weight, left_vector):
@@ -32,7 +38,7 @@
         scatter_dimension=0,
         tiled=True,
     )
-    grad_sum = lax.psum(shard_sum, "dp").astype(jnp.float32)
+    grad_sum = add_all(shard_sum, "dp").astype(jnp.float32)
     entry_count = shard_rows * lax.axis_size("fsdp") * weight.shape[1]
     along_right = jnp.dot(grad_sum, right_next, precision=highest)
     grad_sq_raw, inner_prod, cross_term = lax.psum(

time: 356 us -> 429 us (1.21)
  waiting for transfers between devices: 233 us -> 298 us
  other arithmetic: 10.2 us -> 17.5 us
    all_gather x0 -> x1, waiting for transfers between devices: none -> 124 us  [add_all(): blocks = lax.all_gather(array, axis, axis=0, tiled=False)]
    psum x1 -> x0, waiting for transfers between devices: 51.7 us -> none  [per_device(): grad_sum = lax.psum(shard_sum, 'dp').astype(jnp.float32)]
    reduce_sum x0 -> x1, other arithmetic: none -> 7.2 us  [add_all(): total = blocks.sum(axis=0)]
    all_gather x1, waiting for transfers between devices: 61.3 us -> 55.7 us  [per_device(): gathered = lax.all_gather(weight, 'fsdp', axis=0, tiled=True)]
  transfers between devices with their start and end apart: 3 -> 3, of which waited for: 3 -> 3; matrix products, arithmetic and copies ran while one was open for 5% -> 8% of each run, Pallas kernels for 0% -> 0%
where the time goes in v1:
time: 429 us; the launch traced here: 428 us
  waiting for transfers between devices  298 us (69%)
  matrix products  51.4 us (12%)
  blocking collectives  40.7 us (9%)
  between operations  18.4 us (4%)
  other arithmetic  17.5 us (4%)
    all_gather x1, waiting for transfers between devices, add_all(): blocks = lax.all_gather(array, axis, axis=0, tiled=False)  124 us
    reduce_scatter x1, waiting for transfers between devices, per_device(): lax.psum_scatter(lax.dot_general(tokens, cotangent, (((0,), (0,)), ((), (...  118 us
    all_gather x1, waiting for transfers between devices, per_device(): gathered = lax.all_gather(weight, 'fsdp', axis=0, tiled=True)  55.7 us
    dot_general x1, matrix products, per_device(): lax.dot_general(tokens, cotangent, (((0,), (0,)), ((), ())), preferred_el...  14.6 us
    psum x1, blocking collectives, per_device(): lax.psum((jnp.sum(grad_sum * grad_sum), jnp.sum(grad_sum * weight_wide),...  14.5 us
    dot_general x1, matrix products, per_device(): lax.dot_general(cotangent, gathered, (((1,), (1,)), ((), ())), preferred_...  13.9 us
    dot_general x1, matrix products, per_device(): product = jnp.dot(tokens, gathered, preferred_element_type=jnp.float32)  13.7 us
    psum x1, blocking collectives, per_device(): left_sq = lax.psum(jnp.sum(left_raw * left_raw), 'fsdp')  13.4 us
  transfers between devices with their start and end apart: 3, of which 3 were waited for; matrix products, arithmetic and copies ran while one was open for 8% of the time, Pallas kernels for 0%

profile of v1, /device:TPU:0, one launch (start us, length us, event | category | flops | bytes accessed | tf_op | source)
XLA Modules:
  0.0 428.0 jit_solution(16719236791269977827)
XLA Ops:
  7.2 0.0 copy-start
  7.2 0.0 reduce-scatter.2.cloned.1.call-start
  7.2 1.5 copy-done
  8.8 14.6 %convolution_convert_fusion = bf16[4096,2048]{1,0:T(8,128)(2,1)} fusion(bf16[512,4096]{1,0:T(8,128)(2,1)} %param.4, bf16[512,2048]{1,0:T(8,128)(2,1)S(1)} %copy-done), kind=kOutput, calls=%fused_computation | convolution fusion | flops 8598323200 | bytes 23068672 | tf_op jit(solution)/shard_map/dot_general | solution.py:34
  23.4 0.0 reduce-scatter.2.cloned.1.call-update
  23.4 0.0 copy-start.3
  23.4 0.0 all-gather.4.cloned.1.call-start
  23.5 0.7 all-gather.4.cloned.1.call-update
  24.2 0.0 all-gather.6.cloned.1.call-start
  24.2 118.2 %reduce-scatter.2.cloned.1.call-done = bf16[512,2048]{1,0:T(8,128)(2,1)} async-done(((bf16[4096,2048]{1,0:T(8,128)(2,1)}), bf16[512,2048]{1,0:T(8,128)(2,1)}) %reduce-scatter.2.cloned.1.call-update) | async-done | bytes 2097168 | tf_op jit(solution)/shard_map/reduce_scatter | solution.py:33
  142.5 0.0 all-gather.6.cloned.1.call-update
  142.5 0.0 copy-done.3
  142.5 2.5 fusion.5
  145.0 12.9 %psum.35 = f32[2048]{0:T(1024)S(1)} all-reduce(f32[2048]{0:T(1024)S(1)} %bitcast.22), channel_id=1, replica_groups=mesh['fsdp'=8,'dp'=4] {'fsdp'}, use_global_device_ids=true, to_apply=%region_0.0 | all-reduce | flops 2048 | bytes 16384 | tf_op jit(solution)/shard_map/psum | solution.py:19
  157.9 0.6 multiply_reduce_fusion.1
  159.2 0.6 multiply_reduce_fusion
  159.8 3.3 fusion.6
  163.1 0.6 multiply_reduce_fusion.3
  163.7 13.4 %psum.36 = f32[]{:T(128)} all-reduce(f32[]{:T(128)} %multiply_reduce_fusion.3), channel_id=1, replica_groups=mesh['fsdp'=8,'dp'=4] {'fsdp'}, use_global_device_ids=true, to_apply=%region_3.0 | all-reduce | flops 1 | bytes 8 | tf_op jit(solution)/shard_map/psum | solution.py:22
  178.5 55.7 %all-gather.4.cloned.1.call-done = bf16[4096,2048]{1,0:T(8,128)(2,1)} async-done(((bf16[512,2048]{1,0:T(8,128)(2,1)}), bf16[4096,2048]{1,0:T(8,128)(2,1)}) %all-gather.4.cloned.1.call-update) | async-done | bytes 16777232 | tf_op jit(solution)/shard_map/all_gather | solution.py:25
  234.2 13.9 %divide_convert_fusion = bf16[512,4096]{1,0:T(8,128)(2,1)} fusion(bf16[512,2048]{1,0:T(8,128)(2,1)S(1)} %copy-done, bf16[4096,2048]{1,0:T(8,128)(2,1)} %all-gather.4.cloned.1.call-done, f32[]{:T(128)S(6)} %sqrt.10), kind=kOutput, calls=%fused_computation.1 | convolution fusion | flops 8594128896 | bytes 23068676 | tf_op jit(solution)/shard_map/dot_general | solution.py:28
  248.2 0.0 copy-done.4
  248.2 13.7 %divide_convert_fusion.1 = bf16[512,2048]{1,0:T(8,128)(2,1)} fusion(bf16[512,4096]{1,0:T(8,128)(2,1)S(1)} %copy-done.4, bf16[4096,2048]{1,0:T(8,128)(2,1)} %all-gather.4.cloned.1.call-done, f32[]{:T(128)S(6)} %sqrt.10), kind=kOutput, calls=%fused_computation.10 | convolution fusion | flops 8592031744 | bytes 23068676 | tf_op jit(solution)/shard_map/dot_general | solution.py:26
  261.9 123.6 %all-gather.6.cloned.1.call-done = bf16[2048,2048]{1,0:T(8,128)(2,1)} async-done(((bf16[512,2048]{1,0:T(8,128)(2,1)}), bf16[2048,2048]{1,0:T(8,128)(2,1)}) %all-gather.6.cloned.1.call-update) | async-done | bytes 8388624 | tf_op jit(solution)/shard_map/all_gather | solution.py:10
  385.5 7.2 %reduce_sum.68 = bf16[512,2048]{1,0:T(8,128)(2,1)} reduce(bf16[4,512,2048]{2,1,0:T(8,128)(2,1)} %bitcast.19, bf16[]{:T(256)} %constant.8.clone.1), dimensions={0}, to_apply=%region_5.0 | reduce | flops 3145728 | bytes 10485762 | tf_op jit(solution)/shard_map/reduce_sum | solution.py:11
  392.7 3.3 fusion.7
  396.0 4.1 fusion.2
  400.1 0.6 multiply_reduce_fusion.2
  400.7 14.5 %all-reduce = (f32[]{:T(128)}, f32[]{:T(128)}, f32[]{:T(128)}) all-reduce(f32[]{:T(128)} %get-tuple-element.6, f32[]{:T(128)} %get-tuple-element.5, f32[]{:T(128)} %get-tuple-element.12), channel_id=1, replica_groups=mesh['fsdp'=8,'dp'=4] {'fsdp'}, use_global_device_ids=true, to_apply=%region_9.0 | all-reduce | flops 3 | bytes 24 | tf_op jit(solution)/shard_map/psum | solution.py:44
  417.8 0.0 copy-done.1
  417.8 3.7 fusion.4
  421.5 0.0 copy-done.2
  (4 shorter events, 0.0 us)
Async XLA Ops:
  7.2 1.6 copy-start
  7.2 135.3 %reduce-scatter.2.cloned.1.call-start = ((), (), s32[]{:S(2)}) async-start(), calls=%async_computation.2 | async-start | bytes 18874368 | tf_op jit(solution)/shard_map/reduce_scatter | solution.py:33
  23.4 119.1 %copy-start.3 = (f32[512]{0:T(512)S(1)}, f32[512]{0:T(512)}, u32[]{:S(2)}) copy-start(f32[512]{0:T(512)} %param.7) | copy-start | bytes 6148
  23.4 210.8 %all-gather.4.cloned.1.call-start = ((), (), s32[]{:S(2)}) async-start(), calls=%async_computation.1 | async-start | bytes 18874368 | tf_op jit(solution)/shard_map/all_gather | solution.py:25
  24.2 361.3 %all-gather.6.cloned.1.call-start = ((), (), s32[]{:S(2)}) async-start(), calls=%async_computation.3 | async-start | bytes 10485760 | tf_op jit(solution)/shard_map/all_gather | solution.py:10
  159.8 258.0 %copy-start.1 = (f32[2048]{0:T(1024)}, f32[2048]{0:T(1024)S(1)}, u32[]{:S(2)}) copy-start(f32[2048]{0:T(1024)S(1)} %get-tuple-element.11) | copy-start | bytes 24580
  234.2 13.9 %copy-start.4 = (bf16[512,4096]{1,0:T(8,128)(2,1)S(1)}, bf16[512,4096]{1,0:T(8,128)(2,1)}, u32[]{:S(2)}) copy-start(bf16[512,4096]{1,0:T(8,128)(2,1)} %param.4) | copy-start | bytes 12582916
  400.7 20.8 %copy-start.2 = (f32[512]{0:T(512)}, f32[512]{0:T(512)S(1)}, u32[]{:S(2)}) copy-start(f32[512]{0:T(512)S(1)} %get-tuple-element.13) | copy-start | bytes 6148
Sparse Core Ops, SparseCore 0:
  23.5 118.8 reduce-scatter.1
  144.3 89.8 all-gather.3
  235.8 149.5 all-gather.5
